TPU v7x, 32 devices: a whole 2x2x4 slice. The times are simulated.
32 devices in a mesh: grp: 2 (over x), dev: 16 (over z, y, core).
Axes of the slice: x: 2, y: 2, z: 4, core: 2. Of those that a mesh axis runs over, the one named last changes fastest.
Arguments:
- line_bin: int32 [65536], P(('grp', 'dev')), may hold values from 0 to 16383, as said below
- line_slot: int32 [65536], P(('grp', 'dev')), may hold values from 0 to 31
- strength: float32 [65536], P(('grp', 'dev')), may hold values from 0.05 to 1
- line_count: int32 [32], P(('grp', 'dev')), may hold values from 1024 to 2048
- gauss_width: float32 [32], replicated, may hold values from 2 to 40
- lorentz_width: float32 [32], replicated, may hold values from 1 to 30
- mixing: float32 [32], replicated, may hold values from 0.1 to 0.9
- profile_factor: float32 [32, 257], replicated, may hold values from 0.25 to 1.75
Outputs:
- spectrum: float32 [32768], P(('grp', 'dev'))
Inputs may be any that keep to these rules, and one draw needn't show every extreme that they name: `line_bin`: every line of device (g, d) (the d-th block of 2048 lines within the g-th group of 16 blocks) has a bin within (d - 2) * 1024 to (d + 3) * 1024 - 1 of its super-band.
All inputs are finite; a program needn't handle non-finite values.
Results may differ from a plain program's by a relative error of at most 0.00005.
Values sent between devices are 32-bit elements; how exact they have to be, the bound alone decides.
No kernel may reach another device: no remote copies, remote signals or barrier semaphores. Data moves between devices by JAX's collectives and lax.ppermute only.
A program may use at most 64 MiB of HBM per device.

v0:
```python
import jax
import jax.numpy as jnp
from jax import lax
from jax.sharding import PartitionSpec as P

SLOTS = 32
WING = 128
HOP = 2
SPAN = 1024


def shifted(value, axis, by):
    devices = lax.axis_size(axis)
    pairs = [(i, i + by) for i in range(devices) if 0 <= i + by < devices]
    return lax.ppermute(value, axis, pairs)


def padded_2(value, sides, width):
    for axis, dim in sides:
        devices, length = (lax.axis_size(axis), value.shape[dim])
        up = [(i, (i + 1) % devices) for i in range(devices - 1)]
        down = [(j, i) for i, j in up]
        last = lax.slice_in_dim(value, length - width, length, axis=dim)
        first = lax.slice_in_dim(value, 0, width, axis=dim)
        before = lax.ppermute(last, axis, up)
        after = lax.ppermute(first, axis, down)
        value = jnp.concatenate([before, value, after], axis=dim)
    return value


def build_kernel(gauss_width, lorentz_width, mixing, profile_factor):
    offset = jnp.arange(-WING, WING + 1).astype(jnp.float32)
    square = offset[None, :] * offset[None, :]
    lorentz = (
        lorentz_width[:, None]
        * lorentz_width[:, None]
        / (square + lorentz_width[:, None] * lorentz_width[:, None])
    )
    gauss = jnp.exp(-square / (2.0 * gauss_width[:, None] * gauss_width[:, None]))
    raw = (mixing[:, None] * lorentz + (1.0 - mixing[:, None]) * gauss) * profile_factor
    return raw / jnp.sum(raw, axis=1, keepdims=True)


def convolve_padded(padded, kernel):
    spread = lax.conv_general_dilated(
        padded[None],
        kernel[:, None, :],
        (1,),
        [(0, 0)],
        feature_group_count=SLOTS,
        precision=lax.Precision.HIGHEST,
    )
    return jnp.sum(spread[0], axis=0)


def body(
    line_bin, line_slot, strength, line_count, gauss_width, lorentz_width, mixing, profile_factor
):
    lines = line_bin.shape[0]
    span_cells = SPAN
    reach = 2 * HOP + 1
    width = reach * span_cells
    anchor = (lax.axis_index("dev") - HOP) * span_cells
    live = jnp.arange(lines) < line_count[0]
    weight = jnp.where(live, strength, jnp.float32(0.0))
    flat = line_slot * width + (line_bin - anchor)
    grid = jnp.zeros((SLOTS * width,), jnp.float32).at[flat].add(weight).reshape(SLOTS, width)
    kernel = build_kernel(gauss_width, lorentz_width, mixing, profile_factor)
    blocks = grid.reshape(SLOTS, reach, span_cells)
    carried_low = blocks[:, 0]
    for step in range(1, HOP + 1):
        carried_low = shifted(carried_low, "dev", -1) + blocks[:, step]
    carried_high = blocks[:, 2 * HOP]
    for step in range(1, HOP + 1):
        carried_high = shifted(carried_high, "dev", 1)
        if step < HOP:
            carried_high = carried_high + blocks[:, 2 * HOP - step]
    owned = carried_low + carried_high
    padded = padded_2(owned, ((("grp", "dev"), 1),), WING)
    return convolve_padded(padded, kernel)


def solution(mesh):
    in_specs = (
        P(("grp", "dev")),
        P(("grp", "dev")),
        P(("grp", "dev")),
        P(("grp", "dev")),
        P(),
        P(),
        P(),
        P(),
    )
    out_specs = P(("grp", "dev"))
    return jax.shard_map(body, mesh=mesh, in_specs=in_specs, out_specs=out_specs, check_vma=False)
```

profile of v0, /device:TPU:5, one launch (start us, length us, event | category | flops | bytes accessed | tf_op | source)
XLA Modules:
  0.0 73.0 jit_solution(8787608626693763226)
XLA Ops:
  0.0 0.0 copy-start.3
  0.7 0.0 copy-done.3
  0.7 0.0 copy-start.1
  0.7 0.0 copy-start.2
  0.7 0.7 copy-done.1
  1.4 0.0 copy-done.2
  1.4 11.4 %scatter_custom_fusion = f32[163840]{0:T(1024)S(1)} fusion(s32[2048]{0:T(1024)S(1)} %compare_select_fusion, f32[2048]{0:T(1024)S(1)} %fusion.8, f32[]{:T(128)} %constant.10.clone.1), kind=kCustom, calls=%fused_computation.2 | custom fusion | flops 2048 | bytes 655364 | tf_op jit(solution)/shard_map/scatter-add | solution.py:67
  12.8 0.1 reshape_reshape.3
  12.9 0.5 fusion.12
  13.5 2.6 %collective-permute-start = (f32[32,1024]{1,0:T(8,128)S(1)}, f32[32,1024]{1,0:T(8,128)S(1)}, u32[]{:S(2)}, u32[]{:S(2)}) collective-permute-start(f32[32,1024]{1,0:T(8,128)S(1)} %bitcast.27), channel_id=1, source_target_pairs={{1,0},{2,1},{3,2},{4,3},{5,4},{6,5},{7,6},{8,7},{9,8},{10,9},{11,1... | collective-permute-start | bytes 393224 | tf_op jit(solution)/shard_map/ppermute | solution.py:15
  16.1 0.0 copy-start.4
  16.1 0.0 copy-start.5
  16.1 0.0 copy-start.6
  16.1 4.0 %collective-permute-start.2 = (f32[32,1024]{1,0:T(8,128)S(1)}, f32[32,1024]{1,0:T(8,128)S(1)}, u32[]{:S(2)}, u32[]{:S(2)}) collective-permute-start(f32[32,1024]{1,0:T(8,128)S(1)} %bitcast.26), channel_id=1, source_target_pairs={{0,1},{1,2},{2,3},{3,4},{4,5},{5,6},{6,7},{7,8},{8,9},{9,10},{10,1... | collective-permute-start | bytes 393224 | tf_op jit(solution)/shard_map/ppermute | solution.py:15
  20.1 0.0 copy-done.4
  20.2 0.0 copy-done.5
  20.2 0.0 copy-done.6
  20.2 0.5 collective-permute-done
  20.7 1.9 %collective-permute-start.1 = (f32[32,1024]{1,0:T(8,128)S(1)}, f32[32,1024]{1,0:T(8,128)S(1)}, u32[]{:S(2)}, u32[]{:S(2)}) collective-permute-start(f32[32,1024]{1,0:T(8,128)S(1)} %fusion.4), channel_id=1, source_target_pairs={{1,0},{2,1},{3,2},{4,3},{5,4},{6,5},{7,6},{8,7},{9,8},{10,9},{11,1... | collective-permute-start | bytes 393224 | tf_op jit(solution)/shard_map/ppermute | solution.py:15
  22.6 0.0 collective-permute-done.2
  22.6 0.0 copy-start
  22.7 4.7 %collective-permute-start.3 = (f32[32,1024]{1,0:T(8,128)S(1)}, f32[32,1024]{1,0:T(8,128)S(1)}, u32[]{:S(2)}, u32[]{:S(2)}) collective-permute-start(f32[32,1024]{1,0:T(8,128)S(1)} %bitcast_add_fusion), channel_id=1, source_target_pairs={{0,1},{1,2},{2,3},{3,4},{4,5},{5,6},{6,7},{7,8},{8,9},{9,10},{10,1... | collective-permute-start | bytes 393224 | tf_op jit(solution)/shard_map/ppermute | solution.py:15
  27.4 0.0 copy-done
  27.4 0.2 fusion.10
  27.6 0.4 collective-permute-done.1
  28.0 1.3 %collective-permute-done.3 = f32[32,1024]{1,0:T(8,128)S(1)} collective-permute-done((f32[32,1024]{1,0:T(8,128)S(1)}, f32[32,1024]{1,0:T(8,128)S(1)}, u32[]{:S(2)}, u32[]{:S(2)}) %collective-permute-start.3) | collective-permute-done | bytes 131104 | tf_op jit(solution)/shard_map/ppermute | solution.py:15
  29.3 5.3 %collective-permute-start.4 = (f32[32,128]{1,0:T(8,128)S(1)}, f32[32,128]{1,0:T(8,128)S(1)}, u32[]{:S(2)}, u32[]{:S(2)}) collective-permute-start(f32[32,128]{1,0:T(8,128)S(1)} %get-tuple-element.12), channel_id=1, source_target_pairs={{0,1},{1,2},{2,3},{3,4},{4,5},{5,6},{6,7},{7,8},{8,9},{9,10},{10,1... | collective-permute-start | bytes 49160 | tf_op jit(solution)/shard_map/ppermute | solution.py:25
  34.6 1.9 %collective-permute-start.5 = (f32[32,128]{1,0:T(8,128)S(1)}, f32[32,128]{1,0:T(8,128)S(1)}, u32[]{:S(2)}, u32[]{:S(2)}) collective-permute-start(f32[32,128]{1,0:T(8,128)S(1)} %get-tuple-element.13), channel_id=1, source_target_pairs={{1,0},{2,1},{3,2},{4,3},{5,4},{6,5},{7,6},{8,7},{9,8},{10,9},{11,1... | collective-permute-start | bytes 49160 | tf_op jit(solution)/shard_map/ppermute | solution.py:26
  36.5 0.1 divide_bitcast_fusion
  36.6 0.1 copy.21
  36.7 0.0 collective-permute-done.4
  36.7 3.8 %collective-permute-done.5 = f32[32,128]{1,0:T(8,128)S(1)} collective-permute-done((f32[32,128]{1,0:T(8,128)S(1)}, f32[32,128]{1,0:T(8,128)S(1)}, u32[]{:S(2)}, u32[]{:S(2)}) %collective-permute-start.5) | collective-permute-done | bytes 16416 | tf_op jit(solution)/shard_map/ppermute | solution.py:26
  40.6 0.2 copy.20
  40.8 32.2 %convolution_reduce_fusion = f32[1024]{0:T(1024)} fusion(f32[1,32,1280]{1,0,2:T(1,128)S(1)} %bitcast.25, f32[32,1,257]{0,1,2:T(1,128)S(1)} %copy.21), kind=kOutput, calls=%fused_computation.1 | convolution fusion | flops 101088256 | bytes 200832 | tf_op jit(solution)/shard_map/conv_general_dilated | solution.py:45
  (12 shorter events, 0.2 us)
Async XLA Ops:
  0.0 0.7 copy-start.3
  0.7 0.7 copy-start.1
  0.7 0.7 copy-start.2
  13.5 7.2 %collective-permute-start = (f32[32,1024]{1,0:T(8,128)S(1)}, f32[32,1024]{1,0:T(8,128)S(1)}, u32[]{:S(2)}, u32[]{:S(2)}) collective-permute-start(f32[32,1024]{1,0:T(8,128)S(1)} %bitcast.27), channel_id=1, source_target_pairs={{1,0},{2,1},{3,2},{4,3},{5,4},{6,5},{7,6},{8,7},{9,8},{10,9},{11,1... | collective-permute-start | bytes 393224 | tf_op jit(solution)/shard_map/ppermute | solution.py:15
  16.1 4.1 %copy-start.4 = (f32[32]{0:T(128)S(1)}, f32[32]{0:T(128)}, u32[]{:S(2)}) copy-start(f32[32]{0:T(128)} %param.14) | copy-start | bytes 388
  16.1 4.1 %copy-start.5 = (f32[32]{0:T(128)S(1)}, f32[32]{0:T(128)}, u32[]{:S(2)}) copy-start(f32[32]{0:T(128)} %param.12) | copy-start | bytes 388
  16.1 4.1 %copy-start.6 = (f32[32]{0:T(128)S(1)}, f32[32]{0:T(128)}, u32[]{:S(2)}) copy-start(f32[32]{0:T(128)} %param.13) | copy-start | bytes 388
  16.1 6.5 %collective-permute-start.2 = (f32[32,1024]{1,0:T(8,128)S(1)}, f32[32,1024]{1,0:T(8,128)S(1)}, u32[]{:S(2)}, u32[]{:S(2)}) collective-permute-start(f32[32,1024]{1,0:T(8,128)S(1)} %bitcast.26), channel_id=1, source_target_pairs={{0,1},{1,2},{2,3},{3,4},{4,5},{5,6},{6,7},{7,8},{8,9},{9,10},{10,1... | collective-permute-start | bytes 393224 | tf_op jit(solution)/shard_map/ppermute | solution.py:15
  20.7 7.3 %collective-permute-start.1 = (f32[32,1024]{1,0:T(8,128)S(1)}, f32[32,1024]{1,0:T(8,128)S(1)}, u32[]{:S(2)}, u32[]{:S(2)}) collective-permute-start(f32[32,1024]{1,0:T(8,128)S(1)} %fusion.4), channel_id=1, source_target_pairs={{1,0},{2,1},{3,2},{4,3},{5,4},{6,5},{7,6},{8,7},{9,8},{10,9},{11,1... | collective-permute-start | bytes 393224 | tf_op jit(solution)/shard_map/ppermute | solution.py:15
  22.6 4.7 %copy-start = (f32[32,257]{1,0:T(8,128)S(1)}, f32[32,257]{1,0:T(8,128)}, u32[]{:S(2)}) copy-start(f32[32,257]{1,0:T(8,128)} %param.15) | copy-start | bytes 98692
  22.7 6.6 %collective-permute-start.3 = (f32[32,1024]{1,0:T(8,128)S(1)}, f32[32,1024]{1,0:T(8,128)S(1)}, u32[]{:S(2)}, u32[]{:S(2)}) collective-permute-start(f32[32,1024]{1,0:T(8,128)S(1)} %bitcast_add_fusion), channel_id=1, source_target_pairs={{0,1},{1,2},{2,3},{3,4},{4,5},{5,6},{6,7},{7,8},{8,9},{9,10},{10,1... | collective-permute-start | bytes 393224 | tf_op jit(solution)/shard_map/ppermute | solution.py:15
  29.3 7.4 %collective-permute-start.4 = (f32[32,128]{1,0:T(8,128)S(1)}, f32[32,128]{1,0:T(8,128)S(1)}, u32[]{:S(2)}, u32[]{:S(2)}) collective-permute-start(f32[32,128]{1,0:T(8,128)S(1)} %get-tuple-element.12), channel_id=1, source_target_pairs={{0,1},{1,2},{2,3},{3,4},{4,5},{5,6},{6,7},{7,8},{8,9},{9,10},{10,1... | collective-permute-start | bytes 49160 | tf_op jit(solution)/shard_map/ppermute | solution.py:25
  34.6 6.0 %collective-permute-start.5 = (f32[32,128]{1,0:T(8,128)S(1)}, f32[32,128]{1,0:T(8,128)S(1)}, u32[]{:S(2)}, u32[]{:S(2)}) collective-permute-start(f32[32,128]{1,0:T(8,128)S(1)} %get-tuple-element.13), channel_id=1, source_target_pairs={{1,0},{2,1},{3,2},{4,3},{5,4},{6,5},{7,6},{8,7},{9,8},{10,9},{11,1... | collective-permute-start | bytes 49160 | tf_op jit(solution)/shard_map/ppermute | solution.py:26
where the time goes:
time: 73.4 us; the launch traced here: 73 us
  matrix products  32.2 us (44%)
  starting transfers between devices  20.4 us (28%)
  other arithmetic  11.8 us (16%)
  waiting for transfers between devices  5.99 us (8%)
  local copies, waits for them, and re-layouts  1.74 us (2%)
  between operations  0.9 us (1%)
    conv_general_dilated x1, matrix products, convolve_padded(): lax.conv_general_dilated(padded[None], kernel[:, None, :], (1,), [(0, 0)]...  32.2 us
    ppermute x4, starting transfers between devices, shifted(): return lax.ppermute(value, axis, pairs)  13.2 us
    scatter-add x1, other arithmetic, body(): jnp.zeros((SLOTS * width,), jnp.float32).at[flat].add(weight)  11.4 us
    ppermute x1, starting transfers between devices, padded_2(): before = lax.ppermute(last, axis, up)  5.25 us
    ppermute x1, waiting for transfers between devices, padded_2(): after = lax.ppermute(first, axis, down)  3.82 us
    ppermute x4, waiting for transfers between devices, shifted(): return lax.ppermute(value, axis, pairs)  2.17 us
    ppermute x1, starting transfers between devices, padded_2(): after = lax.ppermute(first, axis, down)  1.92 us
  transfers between devices with their start and end apart: 6, of which 4 were waited for; matrix products, arithmetic and copies ran while one was open for 1% of the time, Pallas kernels for 0%

commit v1 on v0

v1 whole, which is shorter than its diff:
```python
import jax
import jax.numpy as jnp
from jax import lax
from jax.experimental import pallas as pl
from jax.experimental.pallas import tpu as pltpu
from jax.sharding import PartitionSpec as P

HOP = 2
SPAN = 1024
LANES = 128
BLOCK = 256
AXES = ("grp", "dev")


def column(row):
    n = row.shape[1]
    here = lax.broadcasted_iota(jnp.int32, (n, n), 0)
    there = lax.broadcasted_iota(jnp.int32, (n, n), 1)
    return jnp.sum(jnp.where(here == there, row, 0.0), axis=1, keepdims=True)


def halves(value):
    high = value.astype(jnp.bfloat16)
    low = (value - high.astype(jnp.float32)).astype(jnp.bfloat16)
    return high, low


def kernel_table(gauss, lorentz, mixing, factor_ref):
    slots = gauss.shape[0]
    wing = (factor_ref.shape[1] - 1) // 2

    def profile(offset, factor):
        square = offset * offset
        width = lorentz * lorentz
        shape = mixing * (width / (square + width)) + (1.0 - mixing) * jnp.exp(
            -square / (2.0 * gauss * gauss)
        )
        return shape * factor

    lane = lax.broadcasted_iota(jnp.int32, (slots, LANES), 1)
    raw = []
    for start in range(0, 2 * wing, LANES):
        offset = (lane + (start - wing)).astype(jnp.float32)
        raw.append(profile(offset, factor_ref[:, start : start + LANES]))
    last = profile(jnp.full((slots, 1), float(wing), jnp.float32), factor_ref[:, 2 * wing :])
    total = sum(jnp.sum(part, axis=1, keepdims=True) for part in raw) + last
    raw.append(jnp.broadcast_to(last, (slots, LANES)))
    return [part / total for part in raw]


def deposit_kernel(
    count_ref, bin_ref, slot_ref, strength_ref, gauss_ref, lorentz_ref, mixing_ref, factor_ref, out_ref
):
    slots = gauss_ref.shape[1]
    pieces = (factor_ref.shape[1] - 1) // LANES
    lines = bin_ref.shape[1]
    reach_rows = (2 * HOP + 1) * SPAN // LANES
    rows = -(-(reach_rows + pieces) // 16) * 16
    bf16 = jnp.bfloat16

    table = kernel_table(
        column(gauss_ref[...]), column(lorentz_ref[...]), column(mixing_ref[...]), factor_ref
    )
    table = jnp.concatenate(table, axis=1)
    high, low = halves(table)
    weights = jnp.concatenate([high, low, high, low], axis=0)
    ones = (lax.broadcasted_iota(jnp.int32, (16, LANES), 0) == 0).astype(jnp.float32).astype(bf16)
    weights = jnp.concatenate(
        [
            jnp.concatenate([weights, jnp.zeros((4 * slots, LANES), bf16)], axis=1),
            jnp.concatenate([jnp.zeros((16, table.shape[1]), bf16), ones], axis=1),
        ],
        axis=0,
    )

    anchor = (lax.axis_index("dev") - HOP) * SPAN
    count = count_ref[0]
    slot_ids = lax.broadcasted_iota(jnp.int32, (slots, BLOCK), 0)
    row_ids = lax.broadcasted_iota(jnp.int32, (rows, BLOCK), 0)
    lane = lax.broadcasted_iota(jnp.int32, (BLOCK, LANES), 1)
    acc = jnp.zeros((rows, 2 * LANES), jnp.float32)
    for start in range(0, lines, BLOCK):
        at = slice(start, start + BLOCK)
        where = bin_ref[:, at] - anchor
        row, col = where >> 7, where & (LANES - 1)
        live = lax.broadcasted_iota(jnp.int32, (1, BLOCK), 1) + start < count
        weight = jnp.where(live, strength_ref[:, at], 0.0)
        chosen = jnp.where(slot_ids == slot_ref[:, at], weight, 0.0)
        chosen_high, chosen_low = halves(chosen)
        cols = jnp.broadcast_to(col.astype(jnp.float32), (16, BLOCK)).astype(bf16)
        picks = jnp.concatenate([chosen_high, chosen_high, chosen_low, chosen_low, cols], axis=0)
        spread = lax.dot_general(
            picks, weights, (((0,), (0,)), ((), ())), preferred_element_type=jnp.float32
        )
        col = spread[:, (pieces + 1) * LANES :].astype(jnp.int32)
        index = (col - lane) & (LANES - 1)
        turned = [
            jnp.take_along_axis(
                spread[:, k * LANES : (k + 1) * LANES], index, axis=1, mode="promise_in_bounds"
            )
            for k in range(pieces)
        ]
        last = spread[:, pieces * LANES : (pieces + 1) * LANES]
        after, here = lane > col, lane == col
        for k in range(pieces + 1):
            if k == 0:
                value = jnp.where(after, turned[pieces - 1], jnp.where(here, last, 0.0))
            elif k == pieces:
                value = jnp.where(after, 0.0, turned[0])
            else:
                value = jnp.where(after, turned[pieces - 1 - k], turned[pieces - k])
            onto = (row_ids == row + k).astype(jnp.float32).astype(bf16)
            acc += jnp.dot(
                onto, jnp.concatenate(halves(value), axis=1), preferred_element_type=jnp.float32
            )
    out_ref[...] = acc[:, :LANES] + acc[:, LANES:]


def local_spectrum(line_bin, line_slot, strength, line_count, gauss, lorentz, mixing, factor):
    lines, slots = line_bin.shape[0], gauss.shape[0]
    pieces = (factor.shape[1] - 1) // LANES
    reach_rows = (2 * HOP + 1) * SPAN // LANES
    rows = -(-(reach_rows + pieces) // 16) * 16
    vmem = pl.BlockSpec(memory_space=pltpu.VMEM)
    return pl.pallas_call(
        deposit_kernel,
        out_shape=jax.ShapeDtypeStruct((rows, LANES), jnp.float32),
        in_specs=[pl.BlockSpec(memory_space=pltpu.SMEM)] + [vmem] * 7,
        out_specs=vmem,
    )(
        line_count,
        line_bin.reshape(1, lines),
        line_slot.reshape(1, lines),
        strength.reshape(1, lines),
        gauss.reshape(1, slots),
        lorentz.reshape(1, slots),
        mixing.reshape(1, slots),
        factor,
    )


def body(line_bin, line_slot, strength, line_count, gauss, lorentz, mixing, factor):
    spectrum = local_spectrum(line_bin, line_slot, strength, line_count, gauss, lorentz, mixing, factor)
    devices = lax.axis_size(AXES)
    me = lax.axis_index(AXES)
    wing_rows = (factor.shape[1] - 1) // 2 // LANES
    span_rows = SPAN // LANES
    far = HOP + 1
    whole = jnp.zeros(((devices + 2 * far) * span_rows, LANES), jnp.float32)
    used = (2 * HOP + 1) * span_rows + 2 * wing_rows
    whole = lax.dynamic_update_slice(
        whole, spectrum[:used], ((me + far - HOP) * span_rows - wing_rows, 0)
    )
    parts = whole[far * span_rows : (far + devices) * span_rows].reshape(devices, span_rows, LANES)
    parts = lax.all_to_all(parts, AXES, 0, 0, tiled=True)
    return jnp.sum(parts, axis=0).reshape(SPAN)


def solution(mesh):
    in_specs = (P(AXES),) * 4 + (P(),) * 4
    return jax.shard_map(body, mesh=mesh, in_specs=in_specs, out_specs=P(AXES), check_vma=False)
```

time: 73.4 us -> 22.1 us (0.30)
  the two profiles are of different devices: /device:TPU:5 before, /device:TPU:0 now
where the time goes in v1:
time: 22.1 us; the launch traced here: 21.9 us
  blocking collectives  15.3 us (69%)
  Pallas kernels  4.22 us (19%)
  local copies, waits for them, and re-layouts  1.05 us (5%)
  between operations  0.67 us (3%)
  other arithmetic  0.63 us (3%)
    all_to_all x1, blocking collectives, body(): parts = lax.all_to_all(parts, AXES, 0, 0, tiled=True)  15.3 us
    pallas_call x1, Pallas kernels, local_spectrum(): pl.pallas_call(deposit_kernel, out_shape=jax.ShapeDtypeStruct((rows, LANE...  4.22 us
    unnamed x2, local copies, waits for them, and re-layouts  0.72 us
    reduce_sum x1, other arithmetic, body(): return jnp.sum(parts, axis=0).reshape(SPAN)  0.63 us

profile of v1, /device:TPU:0, one launch (start us, length us, event | category | flops | bytes accessed | tf_op | source)
XLA Modules:
  0.0 21.9 jit_solution(3055649318130370624)
XLA Ops:
  0.7 4.2 %shard_map.82 = f32[48,128]{1,0:T(8,128)} custom-call(s32[1]{0:T(128)S(6)} %copy.10.count_ref, s32[1,2048]{1,0:T(1,128)} %bitcast.11, s32[1,2048]{1,0:T(1,128)} %bitcast.12, f32[1,2048]{1,0:T(1,128)} %bitcast.13, f32[1,32]{1,0:T(1,128)} %bitcast.14, f32[1,32]{1,0:T(1,128)} %bitcast.15, f32[1,32]{1,0:T(1,128)} %bitcast.16, f32[32,257]{1,0:T(8,128)} %factor_ref.1), custom_call_target="tpu_custom_call" | custom-call | tf_op jit(solution)/shard_map/pallas_call | solution.py:125
  4.9 0.0 copy-start
  4.9 0.7 %copy-done = f32[48,128]{1,0:T(8,128)S(1)} copy-done((f32[48,128]{1,0:T(8,128)S(1)}, f32[48,128]{1,0:T(8,128)}, u32[]{:S(2)}) %copy-start) | copy-done | bytes 24600
  5.6 0.3 %dynamic_update_slice.3 = f32[304,128]{1,0:T(8,128)S(1)} dynamic-update-slice(f32[304,128]{1,0:T(8,128)S(1)} %broadcast_in_dim.3, f32[42,128]{1,0:T(8,128)S(1)} %bitcast.10, s32[]{:T(128)S(6)} %select_n.3, s32[]{:T(128)} %constant.27.clone.1) | dynamic-update-slice | bytes 43012 | tf_op jit(solution)/shard_map/dynamic_update_slice | solution.py:151
  5.9 15.3 %all_to_all.5 = f32[32,8,128]{2,1,0:T(8,128)S(1)} all-to-all(f32[32,8,128]{2,1,0:T(8,128)S(1)} %slice_bitcast_fusion), channel_id=1, replica_groups=mesh['grp'=2,'dev'=16] {'grp','dev'}, dimensions={0} | all-to-all | bytes 262144 | tf_op jit(solution)/shard_map/all_to_all | solution.py:155
  21.2 0.6 %reduce_sum.9 = f32[8,128]{1,0:T(8,128)} reduce(f32[32,8,128]{2,1,0:T(8,128)S(1)} %all_to_all.5, f32[]{:T(128)} %constant.10.clone.1), dimensions={0}, to_apply=%region_0.0 | reduce | flops 31744 | bytes 135172 | tf_op jit(solution)/shard_map/reduce_sum | solution.py:156
  (2 shorter events, 0.0 us)
Async XLA Ops:
  4.9 0.7 %copy-start = (f32[48,128]{1,0:T(8,128)S(1)}, f32[48,128]{1,0:T(8,128)}, u32[]{:S(2)}) copy-start(f32[48,128]{1,0:T(8,128)} %shard_map.82) | copy-start | bytes 73732

commit v2 on v1

--- a/solution.py
+++ b/solution.py
@@ -49,7 +49,7 @@
 
 
 def deposit_kernel(
-    count_ref, bin_ref, slot_ref, strength_ref, gauss_ref, lorentz_ref, mixing_ref, factor_ref, out_ref
+    count_ref, bin_ref, slot_ref, strength_ref, gauss_ref, lorentz_ref, mixing_ref, factor_ref, out_ref, acc_ref
 ):
     slots = gauss_ref.shape[1]
     pieces = (factor_ref.shape[1] - 1) // LANES
@@ -113,20 +113,34 @@
             acc += jnp.dot(
                 onto, jnp.concatenate(halves(value), axis=1), preferred_element_type=jnp.float32
             )
-    out_ref[...] = acc[:, :LANES] + acc[:, LANES:]
+    span_rows, wing_rows = SPAN // LANES, pieces // 2
+    shift = (HOP + 1) * span_rows - HOP * span_rows - wing_rows
+    acc_ref[:shift] = jnp.zeros((shift, LANES), jnp.float32)
+    acc_ref[shift : shift + rows] = acc[:, :LANES] + acc[:, LANES:]
+    end = shift + reach_rows + 2 * wing_rows
+    acc_ref[end:] = jnp.zeros((acc_ref.shape[0] - end, LANES), jnp.float32)
+    out_ref[...] = jnp.zeros_like(out_ref)
+    me = lax.axis_index(AXES)
+    for step in range(-HOP - 1, HOP + 2):
+        at = me + step
+
+        @pl.when((at >= 0) & (at < out_ref.shape[0]))
+        def _():
+            first = (step + HOP + 1) * span_rows
+            out_ref[at] = acc_ref[first : first + span_rows]
 
 
-def local_spectrum(line_bin, line_slot, strength, line_count, gauss, lorentz, mixing, factor):
+def span_blocks(line_bin, line_slot, strength, line_count, gauss, lorentz, mixing, factor):
     lines, slots = line_bin.shape[0], gauss.shape[0]
-    pieces = (factor.shape[1] - 1) // LANES
-    reach_rows = (2 * HOP + 1) * SPAN // LANES
-    rows = -(-(reach_rows + pieces) // 16) * 16
+    span_rows = SPAN // LANES
+    rows = -(-((2 * HOP + 3) * span_rows + LANES) // 16) * 16
     vmem = pl.BlockSpec(memory_space=pltpu.VMEM)
     return pl.pallas_call(
         deposit_kernel,
-        out_shape=jax.ShapeDtypeStruct((rows, LANES), jnp.float32),
+        out_shape=pltpu.VMEM((lax.axis_size(AXES), span_rows, LANES), jnp.float32),
         in_specs=[pl.BlockSpec(memory_space=pltpu.SMEM)] + [vmem] * 7,
         out_specs=vmem,
+        scratch_shapes=[pltpu.VMEM((rows, LANES), jnp.float32)],
     )(
         line_count,
         line_bin.reshape(1, lines),
@@ -140,18 +154,7 @@
 
 
 def body(line_bin, line_slot, strength, line_count, gauss, lorentz, mixing, factor):
-    spectrum = local_spectrum(line_bin, line_slot, strength, line_count, gauss, lorentz, mixing, factor)
-    devices = lax.axis_size(AXES)
-    me = lax.axis_index(AXES)
-    wing_rows = (factor.shape[1] - 1) // 2 // LANES
-    span_rows = SPAN // LANES
-    far = HOP + 1
-    whole = jnp.zeros(((devices + 2 * far) * span_rows, LANES), jnp.float32)
-    used = (2 * HOP + 1) * span_rows + 2 * wing_rows
-    whole = lax.dynamic_update_slice(
-        whole, spectrum[:used], ((me + far - HOP) * span_rows - wing_rows, 0)
-    )
-    parts = whole[far * span_rows : (far + devices) * span_rows].reshape(devices, span_rows, LANES)
+    parts = span_blocks(line_bin, line_slot, strength, line_count, gauss, lorentz, mixing, factor)
     parts = lax.all_to_all(parts, AXES, 0, 0, tiled=True)
     return jnp.sum(parts, axis=0).reshape(SPAN)
 

time: 22.1 us -> 20.4 us (0.923)
  local copies, waits for them, and re-layouts: 1.05 us -> 0 us
  Pallas kernels: 4.22 us -> 3.62 us
    unnamed x2 -> x0, local copies, waits for them, and re-layouts: 0.72 us -> none
    pallas_call x1, Pallas kernels: 4.22 us -> 3.62 us  [span_blocks(): pl.pallas_call(deposit_kernel, out_shape=pltpu.VMEM((lax.axis_size(AXES),...]
    dynamic_update_slice x1 -> x0, local copies, waits for them, and re-layouts: 0.31 us -> none  [body(): lax.dynamic_update_slice(whole, spectrum[:used], ((me + far - HOP) * span...]
where the time goes in v2:
time: 20.4 us; the launch traced here: 20.2 us
  blocking collectives  15.3 us (75%)
  Pallas kernels  3.62 us (18%)
  between operations  0.66 us (3%)
  other arithmetic  0.63 us (3%)
    all_to_all x1, blocking collectives, body(): parts = lax.all_to_all(parts, AXES, 0, 0, tiled=True)  15.3 us
    pallas_call x1, Pallas kernels, span_blocks(): pl.pallas_call(deposit_kernel, out_shape=pltpu.VMEM((lax.axis_size(AXES),...  3.62 us
    reduce_sum x1, other arithmetic, body(): return jnp.sum(parts, axis=0).reshape(SPAN)  0.63 us

profile of v2, /device:TPU:0, one launch (start us, length us, event | category | flops | bytes accessed | tf_op | source)
XLA Modules:
  0.0 20.2 jit_solution(15348782480478631494)
XLA Ops:
  0.7 3.6 %shard_map.82 = f32[32,8,128]{2,1,0:T(8,128)S(1)} custom-call(s32[1]{0:T(128)S(6)} %copy.9.count_ref, s32[1,2048]{1,0:T(1,128)} %bitcast.7, s32[1,2048]{1,0:T(1,128)} %bitcast.8, f32[1,2048]{1,0:T(1,128)} %bitcast.9, f32[1,32]{1,0:T(1,128)} %bitcast.10, f32[1,32]{1,0:T(1,128)} %bitcast.11, f32[1,32]{1,0:T(1,128)} %bitcast.12, f32[32,257]{1,0:T(8,128)} %factor_ref.1), custom_call_target="tpu_custom_call" | custom-call | tf_op jit(solution)/shard_map/pallas_call | solution.py:138
  4.3 15.3 %all_to_all.5 = f32[32,8,128]{2,1,0:T(8,128)S(1)} all-to-all(f32[32,8,128]{2,1,0:T(8,128)S(1)} %shard_map.82), channel_id=1, replica_groups=mesh['grp'=2,'dev'=16] {'grp','dev'}, dimensions={0} | all-to-all | bytes 262144 | tf_op jit(solution)/shard_map/all_to_all | solution.py:158
  19.6 0.6 %reduce_sum.9 = f32[8,128]{1,0:T(8,128)} reduce(f32[32,8,128]{2,1,0:T(8,128)S(1)} %all_to_all.5, f32[]{:T(128)} %constant.0.clone.1), dimensions={0}, to_apply=%region_0.0 | reduce | flops 31744 | bytes 135172 | tf_op jit(solution)/shard_map/reduce_sum | solution.py:159

commit v3 on v2

v3 whole, which is shorter than its diff:
```python
import jax
import jax.numpy as jnp
from jax import lax
from jax.experimental import pallas as pl
from jax.experimental.pallas import tpu as pltpu
from jax.sharding import PartitionSpec as P

HOP = 2
SPAN = 1024
LANES = 128
BLOCK = 256
STAGE = 256
AXES = ("grp", "dev")


def column(row):
    n = row.shape[1]
    here = lax.broadcasted_iota(jnp.int32, (n, n), 0)
    there = lax.broadcasted_iota(jnp.int32, (n, n), 1)
    return jnp.sum(jnp.where(here == there, row, 0.0), axis=1, keepdims=True)


def halves(value):
    high = value.astype(jnp.bfloat16)
    low = (value - high.astype(jnp.float32)).astype(jnp.bfloat16)
    return high, low


def pick_lanes(value, index):
    numbers = lax.GatherDimensionNumbers(
        offset_dims=(),
        collapsed_slice_dims=(1,),
        start_index_map=(1,),
        operand_batching_dims=(0,),
        start_indices_batching_dims=(0,),
    )
    return lax.gather(
        value, index[..., None], numbers, (1, 1), mode=lax.GatherScatterMode.PROMISE_IN_BOUNDS
    )


def kernel_table(gauss, lorentz, mixing, factor_ref):
    slots = gauss.shape[0]
    wing = (factor_ref.shape[1] - 1) // 2

    def profile(offset, factor):
        square = offset * offset
        width = lorentz * lorentz
        shape = mixing * (width / (square + width)) + (1.0 - mixing) * jnp.exp(
            -square / (2.0 * gauss * gauss)
        )
        return shape * factor

    lane = lax.broadcasted_iota(jnp.int32, (slots, LANES), 1)
    raw = []
    for start in range(0, 2 * wing, LANES):
        offset = (lane + (start - wing)).astype(jnp.float32)
        raw.append(profile(offset, factor_ref[:, start : start + LANES]))
    last = profile(jnp.full((slots, 1), float(wing), jnp.float32), factor_ref[:, 2 * wing :])
    total = sum(jnp.sum(part, axis=1, keepdims=True) for part in raw) + last
    return jnp.concatenate(raw, axis=1) / total, last / total


def deposit_kernel(
    count_ref, bin_ref, slot_ref, strength_ref, gauss_ref, lorentz_ref, mixing_ref, factor_ref, give_ref, half_ref, acc_ref, spread_ref
):
    slots = gauss_ref.shape[1]
    pieces = (factor_ref.shape[1] - 1) // LANES
    lines = bin_ref.shape[1]
    reach_rows = (2 * HOP + 1) * SPAN // LANES
    rows = -(-(reach_rows + pieces) // 16) * 16
    bf16 = jnp.bfloat16

    table, last = kernel_table(
        column(gauss_ref[...]), column(lorentz_ref[...]), column(mixing_ref[...]), factor_ref
    )
    high, low = halves(table)
    weights = jnp.concatenate([high, low, high, low], axis=0)
    aux = lax.broadcasted_iota(jnp.int32, (16, LANES), 0)
    aux_lane = lax.broadcasted_iota(jnp.int32, (16, LANES), 1)
    steps = jnp.where(aux == 0, 1, jnp.where(aux == 1, LANES - aux_lane, 0))
    steps = steps.astype(jnp.float32).astype(bf16)
    weights = jnp.concatenate(
        [
            jnp.concatenate([weights, jnp.zeros((4 * slots, LANES), bf16)], axis=1),
            jnp.concatenate([jnp.zeros((16, table.shape[1]), bf16), steps], axis=1),
        ],
        axis=0,
    )

    anchor = (lax.axis_index("dev") - HOP) * SPAN
    count = count_ref[0]
    slot_ids = lax.broadcasted_iota(jnp.int32, (slots, STAGE), 0)
    row_ids = lax.broadcasted_iota(jnp.int32, (rows, BLOCK), 0)
    aux_ids = lax.broadcasted_iota(jnp.int32, (16, STAGE), 0)
    zero, one = jnp.zeros((BLOCK, LANES), bf16), jnp.ones((BLOCK, LANES), bf16)
    ends_at = []
    for start in range(0, lines, STAGE):
        at = slice(start, start + STAGE)
        col = (bin_ref[:, at] - anchor) & (LANES - 1)
        live = lax.broadcasted_iota(jnp.int32, (1, STAGE), 1) + start < count
        weight = jnp.where(live, strength_ref[:, at], 0.0)
        chosen = jnp.where(slot_ids == slot_ref[:, at], weight, 0.0)
        ends_at.append(jnp.sum(chosen * last, axis=0, keepdims=True))
        chosen_high, chosen_low = halves(chosen)
        aux = jnp.where(aux_ids == 0, col, jnp.where(aux_ids == 1, 1, 0))
        aux = aux.astype(jnp.float32).astype(bf16)
        picks = jnp.concatenate([chosen_high, chosen_high, chosen_low, chosen_low, aux], axis=0)
        spread_ref[at, :] = lax.dot_general(
            picks, weights, (((0,), (0,)), ((), ())), preferred_element_type=jnp.float32
        )
    ends_at = jnp.concatenate(ends_at, axis=1)
    acc = jnp.zeros((rows, 2 * LANES), jnp.float32)
    ends = jnp.zeros((2 * rows, LANES), jnp.float32)
    for start in range(0, lines, BLOCK):
        at = slice(start, start + BLOCK)
        row = (bin_ref[:, at] - anchor) >> 7
        step = spread_ref[at, pieces * LANES :]
        index = step.astype(jnp.int32) & (LANES - 1)
        turned = [
            halves(pick_lanes(spread_ref[at, k * LANES : (k + 1) * LANES], index))
            for k in range(pieces)
        ]
        step = step.astype(bf16)
        after, here = step < LANES, step == LANES
        for k in range(pieces + 1):
            past = turned[pieces - 1 - k] if k < pieces else (zero, zero)
            upto = turned[pieces - k] if k > 0 else (zero, zero)
            value = [jnp.where(after, a, b) for a, b in zip(past, upto)]
            onto = (row_ids == row + k).astype(jnp.float32).astype(bf16)
            acc += jnp.dot(
                onto, jnp.concatenate(value, axis=1), preferred_element_type=jnp.float32
            )
        onto = jnp.concatenate(halves(jnp.where(row_ids == row, ends_at[:, at], 0.0)), axis=0)
        ends += jnp.dot(onto, jnp.where(here, one, zero), preferred_element_type=jnp.float32)
    acc = acc[:, :LANES] + acc[:, LANES:] + ends[:rows] + ends[rows:]

    span_rows, wing_rows = SPAN // LANES, pieces // 2
    shift = (HOP + 1) * span_rows - HOP * span_rows - wing_rows
    acc_ref[:shift] = jnp.zeros((shift, LANES), jnp.float32)
    acc_ref[shift : shift + rows] = acc
    end = shift + reach_rows + 2 * wing_rows
    acc_ref[end:] = jnp.zeros((acc_ref.shape[0] - end, LANES), jnp.float32)
    odd = lax.rem(lax.axis_index(AXES), 2)
    far = HOP + 1
    give = pl.multiple_of((1 - odd) * (far + 1) * span_rows, span_rows)
    keep = pl.multiple_of(odd * far * span_rows, span_rows)
    give_ref[...] = acc_ref[pl.ds(give, far * span_rows)]
    half_ref[...] = acc_ref[pl.ds(keep, (far + 1) * span_rows)]


def span_sums(line_bin, line_slot, strength, line_count, gauss, lorentz, mixing, factor):
    lines, slots = line_bin.shape[0], gauss.shape[0]
    span_rows = SPAN // LANES
    rows = -(-((2 * HOP + 3) * span_rows + LANES) // 16) * 16
    vmem = pl.BlockSpec(memory_space=pltpu.VMEM)
    return pl.pallas_call(
        deposit_kernel,
        out_shape=[
            pltpu.VMEM(((HOP + 1) * span_rows, LANES), jnp.float32),
            pltpu.VMEM(((HOP + 2) * span_rows, LANES), jnp.float32),
        ],
        in_specs=[pl.BlockSpec(memory_space=pltpu.SMEM)] + [vmem] * 7,
        out_specs=[vmem] * 2,
        scratch_shapes=[
            pltpu.VMEM((rows, LANES), jnp.float32),
            pltpu.VMEM((lines, factor.shape[1] - 1 + LANES), jnp.float32),
        ],
    )(
        line_count,
        line_bin.reshape(1, lines),
        line_slot.reshape(1, lines),
        strength.reshape(1, lines),
        gauss.reshape(1, slots),
        lorentz.reshape(1, slots),
        mixing.reshape(1, slots),
        factor,
    )


def exchanges(groups, members):
    count = groups * members
    pair = {i: i ^ 1 for i in range(count)}
    near = {i: i + 1 if i % 2 else i - 1 for i in range(count)}
    far = {i: i + 3 if i % 2 else i - 3 for i in range(count)}
    for moves in (near, far):
        for i, j in moves.items():
            if not 0 <= j < count:
                moves[i] = i
    for b in range(members, count, members):
        near.update({b - 3: b, b - 1: b + 1, b: b - 2, b + 2: b - 1})
        far.update({b - 5: b - 1, b - 3: b - 2, b - 1: b - 3, b: b + 2, b + 2: b + 1, b + 4: b})
    for moves in (pair, near, far):
        assert sorted(moves.values()) == list(range(count))
    return [sorted(moves.items()) for moves in (pair, near, far)]


def body(line_bin, line_slot, strength, line_count, gauss, lorentz, mixing, factor):
    groups, members = lax.axis_size("grp"), lax.axis_size("dev")
    pair, near, far = exchanges(groups, members)
    rows = SPAN // LANES
    me, last = lax.axis_index(AXES), groups * members - 1
    group, place = lax.axis_index("grp"), lax.axis_index("dev")
    odd = me % 2 == 1
    even = ~odd

    def before(k):
        return (place == members - k) & (group < groups - 1)

    def behind(k):
        return (place == k) & (group > 0)

    def part(value, first):
        return value[first * rows : (first + 1) * rows]

    give, half = span_sums(line_bin, line_slot, strength, line_count, gauss, lorentz, mixing, factor)
    got = lax.ppermute(give, AXES, pair)
    zero = jnp.zeros((rows, LANES), jnp.float32)
    half = half + jnp.where(
        even, jnp.concatenate([zero, got], axis=0), jnp.concatenate([got, zero], axis=0)
    )
    padded = jnp.concatenate([half, zero], axis=0)
    first = jnp.where(before(3), 3, jnp.where(behind(0), 2, jnp.where(behind(2), 0, 1)))
    to_near = lax.dynamic_slice(padded, (first * rows, 0), (2 * rows, LANES))
    first = jnp.where(before(3) | behind(2), 1, jnp.where(odd, 3, 0))
    to_far = lax.dynamic_slice(padded, (first * rows, 0), (2 * rows, LANES))
    near = lax.ppermute(to_near, AXES, near)
    far = lax.ppermute(to_far, AXES, far)

    inner_even = even & (me > 0) & ~before(2)
    inner_odd = odd & (me < last) & ~before(1)
    outer = before(1) | before(3) | behind(0) | behind(1) | behind(2)
    reached = jnp.where(even, me > 2, me < last - 2) & ~outer
    own = (
        jnp.where(even, part(half, 3), part(half, 0))
        + jnp.where(inner_even | before(1), part(near, 0), 0.0)
        + jnp.where(inner_odd & ~behind(1), part(near, 1), 0.0)
        + jnp.where(reached, part(far, 0), 0.0)
        + jnp.where(behind(1), part(far, 1), 0.0)
    )
    other = (
        jnp.where(inner_odd | before(2), part(near, 0), 0.0)
        + jnp.where(inner_even & ~behind(0), part(near, 1), 0.0)
        + jnp.where(before(1) | behind(0) | behind(1), part(far, 0), 0.0)
        + jnp.where(before(2), part(far, 1), 0.0)
    )
    got = lax.ppermute(other, AXES, pair)
    return (own + got).reshape(SPAN)


def solution(mesh):
    in_specs = (P(AXES),) * 4 + (P(),) * 4
    return jax.shard_map(body, mesh=mesh, in_specs=in_specs, out_specs=P(AXES), check_vma=False)
```

time: 20.4 us -> 19.3 us (0.946)
  the two profiles are of different devices: /device:TPU:0 before, /device:TPU:3 now
where the time goes in v3:
time: 19.3 us; the launch traced here: 19.1 us
  starting transfers between devices  9.63 us (50%)
  waiting for transfers between devices  5.02 us (26%)
  Pallas kernels  3.06 us (16%)
  between operations  0.74 us (4%)
  other arithmetic  0.61 us (3%)
    ppermute x1, starting transfers between devices, body(): near = lax.ppermute(to_near, AXES, near)  3.38 us
    ppermute x1, starting transfers between devices, body(): far = lax.ppermute(to_far, AXES, far)  3.14 us
    pallas_call x1, Pallas kernels, span_sums(): pl.pallas_call(deposit_kernel, out_shape=[pltpu.VMEM(((HOP + 1) * span_ro...  3.06 us
    ppermute x1, starting transfers between devices, body(): got = lax.ppermute(other, AXES, pair)  2.37 us
    ppermute x1, waiting for transfers between devices, body(): far = lax.ppermute(to_far, AXES, far)  1.97 us
    ppermute x1, waiting for transfers between devices, body(): near = lax.ppermute(to_near, AXES, near)  1.39 us
    ppermute x1, waiting for transfers between devices, body(): got = lax.ppermute(give, AXES, pair)  0.83 us
    ppermute x1, waiting for transfers between devices, body(): got = lax.ppermute(other, AXES, pair)  0.82 us
  transfers between devices with their start and end apart: 4, of which 4 were waited for; matrix products, arithmetic and copies ran while one was open for 0% of the time, Pallas kernels for 0%

profile of v3, /device:TPU:3, one launch (start us, length us, event | category | flops | bytes accessed | tf_op | source)
XLA Modules:
  0.0 19.1 jit_solution(11643682543867764902)
XLA Ops:
  0.7 3.1 %shard_map.82 = (f32[24,128]{1,0:T(8,128)S(1)}, f32[32,128]{1,0:T(8,128)S(1)}) custom-call(s32[1]{0:T(128)S(6)} %copy.9.count_ref, s32[1,2048]{1,0:T(1,128)} %bitcast.8, s32[1,2048]{1,0:T(1,128)} %bitcast.9, f32[1,2048]{1,0:T(1,128)} %bitcast.10, f32[1,32]{1,0:T(1,128)} %bitcast.11, f32[1,32]{1,0:T(1,128)} %bitcast.12, f32[1,32]{1,0:T(1,128)} %bitcast.13, ...), custom_call_target="tpu_custom_call" | custom-call | tf_op jit(solution)/shard_map/pallas_call | solution.py:157
  3.7 0.7 %collective-permute-start = (f32[24,128]{1,0:T(8,128)S(1)}, f32[24,128]{1,0:T(8,128)S(1)}, u32[]{:S(2)}, u32[]{:S(2)}) collective-permute-start(f32[24,128]{1,0:T(8,128)S(1)} %get-tuple-element.8), channel_id=1, source_target_pairs={{0,1},{1,0},{2,3},{3,2},{4,5},{5,4},{6,7},{7,6},{8,9},{9,8},{10,11... | collective-permute-start | bytes 36872 | tf_op jit(solution)/shard_map/ppermute | solution.py:217
  4.5 0.8 %collective-permute-done = f32[24,128]{1,0:T(8,128)S(1)} collective-permute-done((f32[24,128]{1,0:T(8,128)S(1)}, f32[24,128]{1,0:T(8,128)S(1)}, u32[]{:S(2)}, u32[]{:S(2)}) %collective-permute-start) | collective-permute-done | bytes 12320 | tf_op jit(solution)/shard_map/ppermute | solution.py:217
  5.3 3.4 %collective-permute-start.1 = (f32[16,128]{1,0:T(8,128)S(1)}, f32[16,128]{1,0:T(8,128)S(1)}, u32[]{:S(2)}, u32[]{:S(2)}) collective-permute-start(f32[16,128]{1,0:T(8,128)S(1)} %get-tuple-element.9), channel_id=1, source_target_pairs={{0,0},{1,2},{2,1},{3,4},{4,3},{5,6},{6,5},{7,8},{8,7},{9,10},{10,9... | collective-permute-start | bytes 24584 | tf_op jit(solution)/shard_map/ppermute | solution.py:227
  8.7 3.1 %collective-permute-start.2 = (f32[16,128]{1,0:T(8,128)S(1)}, f32[16,128]{1,0:T(8,128)S(1)}, u32[]{:S(2)}, u32[]{:S(2)}) collective-permute-start(f32[16,128]{1,0:T(8,128)S(1)} %get-tuple-element.10), channel_id=1, source_target_pairs={{0,0},{1,4},{2,2},{3,6},{4,1},{5,8},{6,3},{7,10},{8,5},{9,12},{10,... | collective-permute-start | bytes 24584 | tf_op jit(solution)/shard_map/ppermute | solution.py:228
  11.9 1.4 %collective-permute-done.1 = f32[16,128]{1,0:T(8,128)S(1)} collective-permute-done((f32[16,128]{1,0:T(8,128)S(1)}, f32[16,128]{1,0:T(8,128)S(1)}, u32[]{:S(2)}, u32[]{:S(2)}) %collective-permute-start.1) | collective-permute-done | bytes 8224 | tf_op jit(solution)/shard_map/ppermute | solution.py:227
  13.3 2.0 %collective-permute-done.2 = f32[16,128]{1,0:T(8,128)S(1)} collective-permute-done((f32[16,128]{1,0:T(8,128)S(1)}, f32[16,128]{1,0:T(8,128)S(1)}, u32[]{:S(2)}, u32[]{:S(2)}) %collective-permute-start.2) | collective-permute-done | bytes 8224 | tf_op jit(solution)/shard_map/ppermute | solution.py:228
  15.3 2.4 %collective-permute-start.3 = (f32[8,128]{1,0:T(8,128)S(1)}, f32[8,128]{1,0:T(8,128)S(1)}, u32[]{:S(2)}, u32[]{:S(2)}) collective-permute-start(f32[8,128]{1,0:T(8,128)S(1)} %select_add_fusion.1), channel_id=1, source_target_pairs={{0,1},{1,0},{2,3},{3,2},{4,5},{5,4},{6,7},{7,6},{8,9},{9,8},{10,11... | collective-permute-start | bytes 12296 | tf_op jit(solution)/shard_map/ppermute | solution.py:247
  17.7 0.8 %collective-permute-done.3 = f32[8,128]{1,0:T(8,128)S(1)} collective-permute-done((f32[8,128]{1,0:T(8,128)S(1)}, f32[8,128]{1,0:T(8,128)S(1)}, u32[]{:S(2)}, u32[]{:S(2)}) %collective-permute-start.3) | collective-permute-done | bytes 4128 | tf_op jit(solution)/shard_map/ppermute | solution.py:247
  18.5 0.6 %fusion.5 = f32[1024]{0:T(1024)} fusion(f32[8,128]{1,0:T(8,128)S(1)} %collective-permute-done.3, f32[32,128]{1,0:T(8,128)S(1)} %select_add_fusion, f32[16,128]{1,0:T(8,128)S(1)} %collective-permute-done.2, f32[16,128]{1,0:T(8,128)S(1)} %collective-permute-done.1, pred[]{:T(512)S(6)} %and.71, pred[]{:T(512)S(6)} %and.73, pred[]{:T(512)S(6)} %and.72, ...), kind=kLoop, calls=%fused_computation.9 | loop fusion | flops 10240 | bytes 32773 | tf_op jit(solution)/shard_map/reshape | solution.py:248
  (3 shorter events, 0.0 us)
Async XLA Ops:
  3.7 1.6 %collective-permute-start = (f32[24,128]{1,0:T(8,128)S(1)}, f32[24,128]{1,0:T(8,128)S(1)}, u32[]{:S(2)}, u32[]{:S(2)}) collective-permute-start(f32[24,128]{1,0:T(8,128)S(1)} %get-tuple-element.8), channel_id=1, source_target_pairs={{0,1},{1,0},{2,3},{3,2},{4,5},{5,4},{6,7},{7,6},{8,9},{9,8},{10,11... | collective-permute-start | bytes 36872 | tf_op jit(solution)/shard_map/ppermute | solution.py:217
  5.3 8.0 %collective-permute-start.1 = (f32[16,128]{1,0:T(8,128)S(1)}, f32[16,128]{1,0:T(8,128)S(1)}, u32[]{:S(2)}, u32[]{:S(2)}) collective-permute-start(f32[16,128]{1,0:T(8,128)S(1)} %get-tuple-element.9), channel_id=1, source_target_pairs={{0,0},{1,2},{2,1},{3,4},{4,3},{5,6},{6,5},{7,8},{8,7},{9,10},{10,9... | collective-permute-start | bytes 24584 | tf_op jit(solution)/shard_map/ppermute | solution.py:227
  8.7 6.6 %collective-permute-start.2 = (f32[16,128]{1,0:T(8,128)S(1)}, f32[16,128]{1,0:T(8,128)S(1)}, u32[]{:S(2)}, u32[]{:S(2)}) collective-permute-start(f32[16,128]{1,0:T(8,128)S(1)} %get-tuple-element.10), channel_id=1, source_target_pairs={{0,0},{1,4},{2,2},{3,6},{4,1},{5,8},{6,3},{7,10},{8,5},{9,12},{10,... | collective-permute-start | bytes 24584 | tf_op jit(solution)/shard_map/ppermute | solution.py:228
  15.3 3.2 %collective-permute-start.3 = (f32[8,128]{1,0:T(8,128)S(1)}, f32[8,128]{1,0:T(8,128)S(1)}, u32[]{:S(2)}, u32[]{:S(2)}) collective-permute-start(f32[8,128]{1,0:T(8,128)S(1)} %select_add_fusion.1), channel_id=1, source_target_pairs={{0,1},{1,0},{2,3},{3,2},{4,5},{5,4},{6,7},{7,6},{8,9},{9,8},{10,11... | collective-permute-start | bytes 12296 | tf_op jit(solution)/shard_map/ppermute | solution.py:247

commit v4 on v3

--- a/solution.py
+++ b/solution.py
@@ -180,28 +180,25 @@
 
 def exchanges(groups, members):
     count = groups * members
-    pair = {i: i ^ 1 for i in range(count)}
-    near = {i: i + 1 if i % 2 else i - 1 for i in range(count)}
-    far = {i: i + 3 if i % 2 else i - 3 for i in range(count)}
-    for moves in (near, far):
-        for i, j in moves.items():
-            if not 0 <= j < count:
-                moves[i] = i
+    pair = [(i, i ^ 1) for i in range(count)]
+    near = [(i, i + (1 if i % 2 else -1)) for i in range(count)]
+    far = [(i, i + (3 if i % 2 else -3)) for i in range(count)]
+    near, far = (
+        [(i, j) for i, j in moves if 0 <= j < count and i // members == j // members]
+        for moves in (near, far)
+    )
+    cross = []
     for b in range(members, count, members):
-        near.update({b - 3: b, b - 1: b + 1, b: b - 2, b + 2: b - 1})
-        far.update({b - 5: b - 1, b - 3: b - 2, b - 1: b - 3, b: b + 2, b + 2: b + 1, b + 4: b})
-    for moves in (pair, near, far):
-        assert sorted(moves.values()) == list(range(count))
-    return [sorted(moves.items()) for moves in (pair, near, far)]
+        cross += [(b - 1, b), (b - 3, b + 1), (b, b - 1), (b + 2, b - 2)]
+    return pair, near, far, cross
 
 
 def body(line_bin, line_slot, strength, line_count, gauss, lorentz, mixing, factor):
     groups, members = lax.axis_size("grp"), lax.axis_size("dev")
-    pair, near, far = exchanges(groups, members)
+    pair, near, far, cross = exchanges(groups, members)
     rows = SPAN // LANES
-    me, last = lax.axis_index(AXES), groups * members - 1
     group, place = lax.axis_index("grp"), lax.axis_index("dev")
-    odd = me % 2 == 1
+    odd = place % 2 == 1
     even = ~odd
 
     def before(k):
@@ -219,31 +216,18 @@
     half = half + jnp.where(
         even, jnp.concatenate([zero, got], axis=0), jnp.concatenate([got, zero], axis=0)
     )
-    padded = jnp.concatenate([half, zero], axis=0)
-    first = jnp.where(before(3), 3, jnp.where(behind(0), 2, jnp.where(behind(2), 0, 1)))
-    to_near = lax.dynamic_slice(padded, (first * rows, 0), (2 * rows, LANES))
-    first = jnp.where(before(3) | behind(2), 1, jnp.where(odd, 3, 0))
-    to_far = lax.dynamic_slice(padded, (first * rows, 0), (2 * rows, LANES))
-    near = lax.ppermute(to_near, AXES, near)
-    far = lax.ppermute(to_far, AXES, far)
-
-    inner_even = even & (me > 0) & ~before(2)
-    inner_odd = odd & (me < last) & ~before(1)
-    outer = before(1) | before(3) | behind(0) | behind(1) | behind(2)
-    reached = jnp.where(even, me > 2, me < last - 2) & ~outer
-    own = (
-        jnp.where(even, part(half, 3), part(half, 0))
-        + jnp.where(inner_even | before(1), part(near, 0), 0.0)
-        + jnp.where(inner_odd & ~behind(1), part(near, 1), 0.0)
-        + jnp.where(reached, part(far, 0), 0.0)
-        + jnp.where(behind(1), part(far, 1), 0.0)
-    )
-    other = (
-        jnp.where(inner_odd | before(2), part(near, 0), 0.0)
-        + jnp.where(inner_even & ~behind(0), part(near, 1), 0.0)
-        + jnp.where(before(1) | behind(0) | behind(1), part(far, 0), 0.0)
-        + jnp.where(before(2), part(far, 1), 0.0)
-    )
+    to_cross = jnp.where(
+        before(3),
+        part(half, 3),
+        jnp.where(before(1), part(half, 1), jnp.where(behind(0), part(half, 2), part(half, 0))),
+    )
+    cross = lax.ppermute(to_cross, AXES, cross)
+    near = lax.ppermute(half[rows : 3 * rows], AXES, near)
+    far = lax.ppermute(jnp.where(even, part(half, 0), part(half, 3)), AXES, far)
+    edge = before(1) | behind(0)
+    own = jnp.where(even, part(half, 3) + part(near, 0), part(half, 0) + part(near, 1))
+    own = own + far + jnp.where(edge, cross, 0.0)
+    other = jnp.where(even, part(near, 1), part(near, 0)) + jnp.where(edge, 0.0, cross)
     got = lax.ppermute(other, AXES, pair)
     return (own + got).reshape(SPAN)
 

time: 19.3 us -> 17.8 us (0.922)
  starting transfers between devices: 9.63 us -> 7.98 us
    ppermute x1, starting transfers between devices: 2.37 us -> 0.07 us  [body(): got = lax.ppermute(other, AXES, pair)]
    ppermute x2 -> x3, starting transfers between devices: 6.52 us -> 7.17 us  [the longest x1 3.37 us: body(): near = lax.ppermute(half[rows:3 * rows], AXES, near)]
    ppermute x1, waiting for transfers between devices: 0.82 us -> 1.14 us  [body(): got = lax.ppermute(other, AXES, pair)]
    ppermute x2 -> x3, waiting for transfers between devices: 3.36 us -> 3.23 us  [the longest x1 3.23 us: body(): cross = lax.ppermute(to_cross, AXES, cross)]
  transfers between devices with their start and end apart: 4 -> 5, of which waited for: 4 -> 3; matrix products, arithmetic and copies ran while one was open for 0% -> 0% of each run, Pallas kernels for 0% -> 0%
where the time goes in v4:
time: 17.8 us; the launch traced here: 17.6 us
  starting transfers between devices  7.98 us (45%)
  waiting for transfers between devices  5.21 us (29%)
  Pallas kernels  3.06 us (17%)
  between operations  0.72 us (4%)
  other arithmetic  0.62 us (3%)
    ppermute x1, starting transfers between devices, body(): near = lax.ppermute(half[rows:3 * rows], AXES, near)  3.37 us
    ppermute x1, waiting for transfers between devices, body(): cross = lax.ppermute(to_cross, AXES, cross)  3.23 us
    pallas_call x1, Pallas kernels, span_sums(): pl.pallas_call(deposit_kernel, out_shape=[pltpu.VMEM(((HOP + 1) * span_ro...  3.06 us
    ppermute x1, starting transfers between devices, body(): far = lax.ppermute(jnp.where(even, part(half, 0), part(half, 3)), AXES, far)  2.51 us
    ppermute x1, starting transfers between devices, body(): cross = lax.ppermute(to_cross, AXES, cross)  1.29 us
    ppermute x1, waiting for transfers between devices, body(): got = lax.ppermute(other, AXES, pair)  1.14 us
    ppermute x1, waiting for transfers between devices, body(): got = lax.ppermute(give, AXES, pair)  0.83 us
    ppermute x1, starting transfers between devices, body(): got = lax.ppermute(give, AXES, pair)  0.74 us
  transfers between devices with their start and end apart: 5, of which 3 were waited for; matrix products, arithmetic and copies ran while one was open for 0% of the time, Pallas kernels for 0%

profile of v4, /device:TPU:3, one launch (start us, length us, event | category | flops | bytes accessed | tf_op | source)
XLA Modules:
  0.0 17.6 jit_solution(10930933696118033642)
XLA Ops:
  0.7 3.1 %shard_map.82 = (f32[24,128]{1,0:T(8,128)S(1)}, f32[32,128]{1,0:T(8,128)S(1)}) custom-call(s32[1]{0:T(128)S(6)} %copy.9.count_ref, s32[1,2048]{1,0:T(1,128)} %bitcast.8, s32[1,2048]{1,0:T(1,128)} %bitcast.9, f32[1,2048]{1,0:T(1,128)} %bitcast.10, f32[1,32]{1,0:T(1,128)} %bitcast.11, f32[1,32]{1,0:T(1,128)} %bitcast.12, f32[1,32]{1,0:T(1,128)} %bitcast.13, ...), custom_call_target="tpu_custom_call" | custom-call | tf_op jit(solution)/shard_map/pallas_call | solution.py:157
  3.7 0.7 %collective-permute-start = (f32[24,128]{1,0:T(8,128)S(1)}, f32[24,128]{1,0:T(8,128)S(1)}, u32[]{:S(2)}, u32[]{:S(2)}) collective-permute-start(f32[24,128]{1,0:T(8,128)S(1)} %get-tuple-element.8), channel_id=1, source_target_pairs={{0,1},{1,0},{2,3},{3,2},{4,5},{5,4},{6,7},{7,6},{8,9},{9,8},{10,11... | collective-permute-start | bytes 36872 | tf_op jit(solution)/shard_map/ppermute | solution.py:214
  4.5 0.8 %collective-permute-done = f32[24,128]{1,0:T(8,128)S(1)} collective-permute-done((f32[24,128]{1,0:T(8,128)S(1)}, f32[24,128]{1,0:T(8,128)S(1)}, u32[]{:S(2)}, u32[]{:S(2)}) %collective-permute-start) | collective-permute-done | bytes 12320 | tf_op jit(solution)/shard_map/ppermute | solution.py:214
  5.3 3.4 %collective-permute-start.1 = (f32[16,128]{1,0:T(8,128)S(1)}, f32[16,128]{1,0:T(8,128)S(1)}, u32[]{:S(2)}, u32[]{:S(2)}) collective-permute-start(f32[16,128]{1,0:T(8,128)S(1)} %slice.35), channel_id=1, source_target_pairs={{1,2},{2,1},{3,4},{4,3},{5,6},{6,5},{7,8},{8,7},{9,10},{10,9},{11,... | collective-permute-start | bytes 24584 | tf_op jit(solution)/shard_map/ppermute | solution.py:225
  8.7 1.3 %collective-permute-start.3 = (f32[8,128]{1,0:T(8,128)S(1)}, f32[8,128]{1,0:T(8,128)S(1)}, u32[]{:S(2)}, u32[]{:S(2)}) collective-permute-start(f32[8,128]{1,0:T(8,128)S(1)} %get-tuple-element.10), channel_id=1, source_target_pairs={{15,16},{13,17},{16,15},{18,14}} | collective-permute-start | bytes 12296 | tf_op jit(solution)/shard_map/ppermute | solution.py:224
  10.0 2.5 %collective-permute-start.2 = (f32[8,128]{1,0:T(8,128)S(1)}, f32[8,128]{1,0:T(8,128)S(1)}, u32[]{:S(2)}, u32[]{:S(2)}) collective-permute-start(f32[8,128]{1,0:T(8,128)S(1)} %get-tuple-element.9), channel_id=1, source_target_pairs={{1,4},{3,6},{4,1},{5,8},{6,3},{7,10},{8,5},{9,12},{10,7},{11,14},{... | collective-permute-start | bytes 12296 | tf_op jit(solution)/shard_map/ppermute | solution.py:226
  12.5 3.2 %collective-permute-done.3 = f32[8,128]{1,0:T(8,128)S(1)} collective-permute-done((f32[8,128]{1,0:T(8,128)S(1)}, f32[8,128]{1,0:T(8,128)S(1)}, u32[]{:S(2)}, u32[]{:S(2)}) %collective-permute-start.3) | collective-permute-done | bytes 4128 | tf_op jit(solution)/shard_map/ppermute | solution.py:224
  15.8 0.0 collective-permute-done.1
  15.8 0.1 collective-permute-start.4
  15.8 0.0 collective-permute-done.2
  15.8 1.1 %collective-permute-done.4 = f32[8,128]{1,0:T(8,128)S(1)} collective-permute-done((f32[8,128]{1,0:T(8,128)S(1)}, f32[8,128]{1,0:T(8,128)S(1)}, u32[]{:S(2)}, u32[]{:S(2)}) %collective-permute-start.4) | collective-permute-done | bytes 4128 | tf_op jit(solution)/shard_map/ppermute | solution.py:231
  17.0 0.6 %add_bitcast_fusion = f32[1024]{0:T(1024)} fusion(f32[8,128]{1,0:T(8,128)S(1)} %collective-permute-done.4, f32[8,128]{1,0:T(8,128)S(1)} %collective-permute-done.3, f32[8,128]{1,0:T(8,128)S(1)} %collective-permute-done.2, f32[16,128]{1,0:T(8,128)S(1)} %collective-permute-done.1, f32[32,128]{1,0:T(8,128)S(1)} %select_add_fusion, pred[]{:T(512)S(6)} %or.3, ...), kind=kLoop, calls=%fused_computation.4 | loop fusion | flops 7168 | bytes 32770 | tf_op jit(solution)/shard_map/reshape | solution.py:232
  (4 shorter events, 0.0 us)
Async XLA Ops:
  3.7 1.6 %collective-permute-start = (f32[24,128]{1,0:T(8,128)S(1)}, f32[24,128]{1,0:T(8,128)S(1)}, u32[]{:S(2)}, u32[]{:S(2)}) collective-permute-start(f32[24,128]{1,0:T(8,128)S(1)} %get-tuple-element.8), channel_id=1, source_target_pairs={{0,1},{1,0},{2,3},{3,2},{4,5},{5,4},{6,7},{7,6},{8,9},{9,8},{10,11... | collective-permute-start | bytes 36872 | tf_op jit(solution)/shard_map/ppermute | solution.py:214
  5.3 10.4 %collective-permute-start.1 = (f32[16,128]{1,0:T(8,128)S(1)}, f32[16,128]{1,0:T(8,128)S(1)}, u32[]{:S(2)}, u32[]{:S(2)}) collective-permute-start(f32[16,128]{1,0:T(8,128)S(1)} %slice.35), channel_id=1, source_target_pairs={{1,2},{2,1},{3,4},{4,3},{5,6},{6,5},{7,8},{8,7},{9,10},{10,9},{11,... | collective-permute-start | bytes 24584 | tf_op jit(solution)/shard_map/ppermute | solution.py:225
  8.7 7.0 %collective-permute-start.3 = (f32[8,128]{1,0:T(8,128)S(1)}, f32[8,128]{1,0:T(8,128)S(1)}, u32[]{:S(2)}, u32[]{:S(2)}) collective-permute-start(f32[8,128]{1,0:T(8,128)S(1)} %get-tuple-element.10), channel_id=1, source_target_pairs={{15,16},{13,17},{16,15},{18,14}} | collective-permute-start | bytes 12296 | tf_op jit(solution)/shard_map/ppermute | solution.py:224
  10.0 5.8 %collective-permute-start.2 = (f32[8,128]{1,0:T(8,128)S(1)}, f32[8,128]{1,0:T(8,128)S(1)}, u32[]{:S(2)}, u32[]{:S(2)}) collective-permute-start(f32[8,128]{1,0:T(8,128)S(1)} %get-tuple-element.9), channel_id=1, source_target_pairs={{1,4},{3,6},{4,1},{5,8},{6,3},{7,10},{8,5},{9,12},{10,7},{11,14},{... | collective-permute-start | bytes 12296 | tf_op jit(solution)/shard_map/ppermute | solution.py:226
  15.8 1.2 %collective-permute-start.4 = (f32[8,128]{1,0:T(8,128)S(1)}, f32[8,128]{1,0:T(8,128)S(1)}, u32[]{:S(2)}, u32[]{:S(2)}) collective-permute-start(f32[8,128]{1,0:T(8,128)S(1)} %select_add_fusion.1), channel_id=1, source_target_pairs={{0,1},{1,0},{2,3},{3,2},{4,5},{5,4},{6,7},{7,6},{8,9},{9,8},{10,11... | collective-permute-start | bytes 12296 | tf_op jit(solution)/shard_map/ppermute | solution.py:231
